TPU v7x, 32 devices: a whole 2x2x4 slice. The times are simulated.
32 devices in a mesh: dp: 8 (over z, x), tensor: 4 (over y, core).
Axes of the slice: x: 2, y: 2, z: 4, core: 2. Of those that a mesh axis runs over, the one named last changes fastest.
Arguments:
- samples: bfloat16 [256, 64], P('dp'), may hold values from -6 to 6
- projections: bfloat16 [256, 256], P('dp'), may hold values from -6 to 6
- weight_in: bfloat16 [64, 2048], P(None, 'tensor'), may hold values from -0.75 to 0.75
- bias_in: bfloat16 [2048], P('tensor'), may hold values from -3 to 3
- weight_mid: bfloat16 [2048, 2048], P('tensor'), may hold values from -0.125 to 0.125
- bias_mid: bfloat16 [2048], replicated, may hold values from -3 to 3
- weight_out: bfloat16 [2048, 64], replicated, may hold values from -0.125 to 0.125
- bias_out: float32 [64], replicated, may hold values from -3 to 3
Outputs:
- sample_loss: float32 [256], P('dp')
- grad_weight_in: float32 [64, 2048], P(None, 'tensor')
- grad_bias_in: float32 [2048], P('tensor')
- grad_weight_mid: float32 [2048, 2048], P(('tensor', 'dp'))
- grad_bias_mid: float32 [2048], P('tensor')
- grad_weight_out: float32 [2048, 64], P('tensor')
- grad_bias_out: float32 [64], replicated
All inputs are finite; a program needn't handle non-finite values.
Results may differ from a plain program's by a relative error of at most 0.01.
Values may be sent and summed in bfloat16 or wider, within the bound.
No kernel may reach another device: no remote copies, remote signals or barrier semaphores. Data moves between devices by JAX's collectives and lax.ppermute only.
A program may use at most 64 MiB of HBM per device.

v0:
```python
import functools

import jax
import jax.numpy as jnp
from jax import lax
from jax.experimental import pallas as pl
from jax.experimental.pallas import tpu as pltpu
from jax.sharding import PartitionSpec as P


VMEM_BYTES = 16 * 2**20
F32 = jnp.float32
BF16 = jnp.bfloat16
NN = (((1,), (0,)), ((), ()))
NT = (((1,), (1,)), ((), ()))
TN = (((0,), (0,)), ((), ()))


def mm(a, b, dims):
    return lax.dot_general(a, b, dims, preferred_element_type=F32)


def stack(parts):
    return jnp.concatenate(parts, axis=0)


def swish_terms(hidden):
    gate = jax.nn.sigmoid(hidden)
    slopes = gate * (1.0 + hidden * (1.0 - gate))
    curv = gate * (1.0 - gate) * (2.0 + hidden * (1.0 - 2.0 * gate))
    return hidden * gate, slopes, curv


def rows_of(full, rows):
    count = full.shape[0] // rows
    return [full[i * rows : (i + 1) * rows] for i in range(count)]


def vectors_of(projections, patch):
    count = projections.shape[1] // patch
    return [projections[:, i * patch : (i + 1) * patch] for i in range(count)]


def input_rows(samples, projections):
    return stack([samples] + vectors_of(projections, samples.shape[1]))


def row_vector(x):
    return x.astype(F32)[None, :]


def forward_layer(pieces, bias):
    act, slopes, curv = swish_terms(pieces[0] + bias)
    layer = stack([act.astype(BF16)] + [(slopes * tan).astype(BF16) for tan in pieces[1:]])
    return layer, slopes, curv


def backward_layer(back, tans, slopes, curv):
    inner = back[1] * tans[0]
    for grad, tan in zip(back[2:], tans[1:]):
        inner = inner + grad * tan
    pre = back[0] * slopes + curv * inner
    signal = stack([pre.astype(BF16)] + [(grad * slopes).astype(BF16) for grad in back[1:]])
    return pre, signal


def first_kernel(ids, samples, projections, w_in, b_in, w_mid, send, keep, w_buf, sems):
    me = ids[0]
    width = w_in.shape[1]
    n_blocks = w_buf.shape[0]
    order = [*range(1, n_blocks, 2), *range(0, n_blocks, 2)]
    copies = []
    for r in order:
        cols = pl.ds(pl.multiple_of((me ^ r) * width, width), width)
        copies.append(pltpu.make_async_copy(w_mid.at[:, cols], w_buf.at[r], sems.at[r]))
        copies[-1].start()
    inputs = input_rows(samples[...], projections[...])
    pieces = rows_of(mm(inputs, w_in[...], NN), samples.shape[0])
    layer = forward_layer(pieces, row_vector(b_in[...]))[0]
    for r, copy in zip(order, copies):
        copy.wait()
        out = send if r % 2 else keep
        out[r // 2] = mm(layer, w_buf[r], NN).astype(BF16)


def score_kernel(ids, samples, projections, h_keep, h_recv, b_mid, w_out, b_out, loss, info, parts):
    me = ids[0]
    patch, width = w_out.shape[0], h_keep.shape[2]
    n_blocks = w_out.shape[1] // width
    rows = projections.shape[0]
    for r in range(n_blocks):
        block = me ^ r
        cols = pl.ds(pl.multiple_of(block * width, width), width)
        h_ref = h_recv if r % 2 else h_keep
        pieces = rows_of(h_ref[r // 2].astype(F32), rows)
        layer = forward_layer(pieces, row_vector(b_mid[cols]))[0]
        parts[block] = mm(layer, w_out[:, cols], NT)
    total = parts[0]
    for b in range(1, n_blocks):
        total = total + parts[b]
    outs = rows_of(total, rows)
    dirs = [v.astype(F32) for v in vectors_of(projections[...], patch)]
    score = outs[0] + row_vector(b_out[...])
    grad = jnp.zeros_like(score)
    losses = jnp.zeros((rows, 1), F32)
    for vec, dscore in zip(dirs, outs[1:]):
        projected = jnp.sum(vec * score, axis=1, keepdims=True)
        traced = jnp.sum(vec * dscore, axis=1, keepdims=True)
        losses = losses + traced + 0.5 * projected * projected
        grad = grad + projected * vec
    diagonal = lax.broadcasted_iota(jnp.int32, (rows, rows), 0) == lax.broadcasted_iota(jnp.int32, (rows, rows), 1)
    loss[...] = jnp.sum(jnp.where(diagonal, losses, 0.0), axis=0, keepdims=True) / len(dirs)
    high = grad.astype(BF16)
    low = (grad - high.astype(F32)).astype(BF16)
    info[...] = jnp.concatenate([high, low, samples[...], projections[...]], axis=1)


def back_kernel(ids, samples, projections, info, h_keep, h_recv, b_mid, w_out, w_mid, w_in, b_in, out):
    me = ids[0]
    patch, width = w_in.shape
    n_blocks = w_out.shape[1] // width
    rows = samples.shape[0]
    inputs = input_rows(samples[...], projections[...])
    out_rows = stack([info[:, :patch], inputs[rows:]])
    back_first = None
    for r in range(n_blocks):
        cols = pl.ds(pl.multiple_of((me ^ r) * width, width), width)
        h_ref = h_recv if r % 2 else h_keep
        pieces = rows_of(h_ref[r // 2].astype(F32), rows)
        _, slopes, curv = swish_terms(pieces[0] + row_vector(b_mid[cols]))
        back = rows_of(mm(out_rows, w_out[:, cols], NN), rows)
        signal = backward_layer(back, pieces[1:], slopes, curv)[1]
        term = mm(signal, w_mid[:, cols], NT)
        back_first = term if back_first is None else back_first + term
    pieces = rows_of(mm(inputs, w_in[...], NN), rows)
    _, slopes, curv = swish_terms(pieces[0] + row_vector(b_in[...]))
    pre, signal = backward_layer(rows_of(back_first, rows), pieces[1:], slopes, curv)
    out[:patch] = mm(inputs, signal, TN).astype(BF16)
    bias = jnp.sum(pre, axis=0, keepdims=True)
    out[patch:] = jnp.broadcast_to(bias, (out.shape[0] - patch, width)).astype(BF16)


def grads_kernel(ids, info, hid, b_mid, w_out, w_sel, block_out, g_out, g_mid, g_bias, acc, acc_mid, acc_bias):
    n_dp, rows, span = info.shape
    patch, width = w_out.shape[0], hid.shape[2]
    n_blocks, part = block_out.shape[0], block_out.shape[1]
    scale = 1.0 / (rows * n_dp * (span // patch - 3))
    cols = pl.ds(pl.multiple_of(ids[0] * width, width), width)
    mask = ids[1] if pairwise_size(n_dp) else 0
    w_own = w_out[:, cols]
    b_own = row_vector(b_mid[cols])
    b_sel = w_sel[patch : patch + 1].astype(F32)
    acc[...] = jnp.zeros_like(acc)
    g_out[...] = jnp.zeros_like(g_out)
    acc_mid[...] = jnp.zeros_like(acc_mid)
    acc_bias[...] = jnp.zeros_like(acc_bias)

    def body(step, carry):
        slot = step ^ mask
        known = info[slot]
        hl = known[:, : 2 * patch]
        inputs = stack(vectors_of(known, patch)[2:])
        out_rows = stack([hl[:, :patch], inputs[rows:]])
        pieces = rows_of(hid[slot].astype(F32), rows)
        layer_two, slopes, curv = forward_layer(pieces, b_own)
        back = rows_of(mm(out_rows, w_own, NN), rows)
        pre, signal = backward_layer(back, pieces[1:], slopes, curv)
        layer_one = forward_layer(rows_of(mm(inputs, w_sel[:patch], NN), rows), b_sel)[0]
        acc[...] += mm(layer_one, signal, TN)
        g_out[...] += mm(out_rows, layer_two, TN)
        acc_mid[...] += pre
        acc_bias[...] += hl.astype(F32)
        return carry

    lax.fori_loop(0, n_dp, body, 0, unroll=n_dp <= 8)
    g_out[...] = g_out[...] * scale
    g_mid[...] = jnp.sum(acc_mid[...], axis=0, keepdims=True) * scale
    both = jnp.sum(acc_bias[...], axis=0, keepdims=True)
    g_bias[...] = (both[:, :patch] + both[:, patch:]) * scale
    for r in range(n_blocks):
        block_out[r] = (acc[r * part : (r + 1) * part] * scale).astype(BF16)


def merge_kernel(scale, ids, *refs):
    me = ids[0]
    *chunks, mine, other, out, g_in, g_bias = refs
    width = mine.shape[1]
    patch = g_in.shape[0]
    for r, ref in enumerate(chunks):
        cols = pl.ds(pl.multiple_of((me ^ r) * width, width), width)
        out[:, cols] = ref[...].astype(F32)
    total = (mine[...].astype(F32) + other[...].astype(F32)) * scale
    g_in[...] = total[:patch]
    g_bias[...] = total[patch : patch + 1]


def shape(dims, dtype):
    return jax.ShapeDtypeStruct(dims, dtype)


def near_shape(dims, dtype):
    return pltpu.VMEM(dims, dtype)


def call(body, out_shape, args, scratch=(), raw=(), near=(), far=()):
    spaces = [pltpu.SMEM] + [pl.ANY if i in raw else pltpu.VMEM for i in range(1, len(args))]
    args = [pltpu.with_memory_space_constraint(a, pltpu.VMEM) if i in near else a for i, a in enumerate(args)]
    args = [pltpu.with_memory_space_constraint(a, pltpu.HBM) if i in far else a for i, a in enumerate(args)]
    return pl.pallas_call(
        body,
        in_specs=[pl.BlockSpec(memory_space=m) for m in spaces],
        out_specs=[pl.BlockSpec(memory_space=pltpu.VMEM)] * len(out_shape),
        out_shape=out_shape,
        scratch_shapes=list(scratch),
        compiler_params=pltpu.CompilerParams(vmem_limit_bytes=VMEM_BYTES),
    )(*args)


def xor_move(x, axis, mask):
    return lax.ppermute(x, axis, [(i, i ^ mask) for i in range(lax.axis_size(axis))])


def pairwise_size(size):
    return size <= 8 and size & (size - 1) == 0


def pairwise(axis):
    return pairwise_size(lax.axis_size(axis))


def doubling_gather(x, axis):
    if not pairwise(axis):
        return lax.all_gather(x, axis)
    out = x[None]
    mask = 1
    while mask < lax.axis_size(axis):
        out = jnp.concatenate([out, xor_move(out, axis, mask)], axis=0)
        mask *= 2
    return out


def bulk_gather(x, axis):
    if not pairwise(axis):
        return lax.all_gather(x, axis)
    size = lax.axis_size(axis)
    slots = {0: x}
    for mask in (2, 4, 6):
        if mask < size:
            slots[mask] = xor_move(x, axis, mask)
    for mask in list(slots):
        slots[mask ^ 1] = xor_move(slots[mask], axis, 1)
    return jnp.stack([slots[i] for i in range(size)], axis=0)


def pair_sum(x, axis):
    if not pairwise(axis):
        return lax.psum(x.astype(F32), axis), jnp.zeros_like(x)
    mask = 1
    while 2 * mask < lax.axis_size(axis):
        x = (x.astype(F32) + xor_move(x, axis, mask).astype(F32)).astype(BF16)
        mask *= 2
    return x, xor_move(x, axis, mask)


def shards(samples, projections, weight_in, bias_in, weight_mid, bias_mid, weight_out, bias_out):
    n_dp, n_t = lax.axis_size("dp"), lax.axis_size("tensor")
    d, t = lax.axis_index("dp"), lax.axis_index("tensor")
    rows, patch = samples.shape
    count = projections.shape[1] // patch
    full = rows * (count + 1)
    width = weight_in.shape[1]
    part = width // n_dp
    scale = 1.0 / (rows * n_dp * count)
    half = n_t // 2
    ids = jnp.stack([t, d]).astype(jnp.int32)
    w_out = weight_out.T

    send, keep = call(
        first_kernel,
        [near_shape((half, full, width), BF16)] * 2,
        (ids, samples, projections, weight_in, bias_in, weight_mid),
        [pltpu.VMEM((n_t, width, width), BF16), pltpu.SemaphoreType.DMA((n_t,))],
        raw=(5,),
        far=(1, 2, 3, 4, 5),
    )

    got = xor_move(send, "tensor", 1)
    chip = [(keep[i].astype(F32) + got[i].astype(F32)).astype(BF16) for i in range(half)]
    chip = lax.optimization_barrier(chip)
    hidden = [c.astype(F32) for c in chip]
    for q in range(1, half):
        for i in range(half):
            hidden[i] = hidden[i] + xor_move(chip[i ^ q], "tensor", 2 * q).astype(F32)
    own = hidden[0].astype(BF16)
    h_keep = jnp.stack([h.astype(BF16) for h in hidden], axis=0)
    h_recv = xor_move(h_keep, "tensor", 1)

    sel = jnp.concatenate([weight_in, bias_in[None, :], jnp.zeros((15, width), BF16)], axis=0)
    sel = doubling_gather(lax.dynamic_slice_in_dim(sel, d * part, part, 1), "tensor")
    w_sel = jnp.concatenate([sel[r] for r in range(n_t)], axis=1)

    hid_all = bulk_gather(own, "dp")

    loss, info = call(
        score_kernel,
        [shape((1, rows), F32), near_shape((rows, (3 + count) * patch), BF16)],
        (ids, samples, projections, h_keep, h_recv, bias_mid, w_out, bias_out),
        [pltpu.VMEM((n_t, full, patch), F32)],
        near=(3, 4, 6),
    )
    info_all = doubling_gather(info, "dp")

    (summed,) = call(
        back_kernel,
        [near_shape((patch + 16, width), BF16)],
        (ids, samples, projections, info, h_keep, h_recv, bias_mid, w_out, weight_mid, weight_in, bias_in),
        near=(3, 4, 5, 7, 8),
    )

    mid_block, g_out, g_mid, g_bias = call(
        grads_kernel,
        [near_shape((n_t, part, width), BF16), shape((patch, width), F32), shape((1, width), F32), shape((1, patch), F32)],
        (ids, info_all, hid_all, bias_mid, w_out, w_sel),
        [pltpu.VMEM((n_t * part, width), F32), pltpu.VMEM((rows, width), F32), pltpu.VMEM((rows, 2 * patch), F32)],
        near=(1, 2, 4, 5) if pairwise("dp") else (),
    )

    chunks = [mid_block[0]] + [xor_move(mid_block[r], "tensor", r) for r in range(1, n_t)]
    grad_mid, g_in, g_bias_in = call(
        functools.partial(merge_kernel, scale),
        [shape((part, n_t * width), F32), shape((patch, width), F32), shape((1, width), F32)],
        (ids, *chunks, *pair_sum(summed, "dp")),
        near=tuple(range(1, n_t + 3)),
    )
    return (
        loss.reshape(rows),
        g_in,
        g_bias_in.reshape(width),
        grad_mid,
        g_mid.reshape(width),
        g_out.T,
        g_bias.reshape(patch),
    )


def solution(mesh):
    placed = (
        P("dp", None),
        P("dp", None),
        P(None, "tensor"),
        P("tensor"),
        P("tensor", None),
        P(),
        P(),
        P(),
    )

    return jax.shard_map(
        shards,
        mesh=mesh,
        in_specs=placed,
        out_specs=(
            P("dp"),
            P(None, "tensor"),
            P("tensor"),
            P(("tensor", "dp"), None),
            P("tensor"),
            P("tensor", None),
            P(),
        ),
        check_vma=False,
    )
```

profile of v0, /device:TPU:0, one launch (start us, length us, event | category | flops | bytes accessed | tf_op | source)
XLA Modules:
  0.0 67.5 jit_solution(4193745060643898673)
XLA Ops:
  0.7 3.0 %shard_map.135 = (bf16[2,160,512]{2,1,0:T(8,128)(2,1)S(1)}, bf16[2,160,512]{2,1,0:T(8,128)(2,1)S(1)}) custom-call(s32[2]{0:T(128)S(1)} %pad_add_fusion.ids, bf16[32,64]{1,0:T(8,128)(2,1)} %samples.5, bf16[32,256]{1,0:T(8,128)(2,1)} %projections.5, bf16[64,512]{1,0:T(8,128)(2,1)} %w_in.3, bf16[512]{0:T(512)(128)(2,1)} %b_in.3, bf16[512,2048]{1,0:T(8,128)(2,1)} %w_mid.3), custom_call_target="tpu_custom_call" | custom-call | tf_op jit(solution)/shard_map/pallas_call | solution.py:209
  5.7 2.8 %collective-permute-start.15 = (bf16[2,80,64]{2,1,0:T(8,128)(2,1)S(1)}, bf16[2,80,64]{2,1,0:T(8,128)(2,1)S(1)}, u32[]{:S(2)}, u32[]{:S(2)}) collective-permute-start(bf16[2,80,64]{2,1,0:T(8,128)(2,1)S(1)} %pad_maximum_fusion.4), channel_id=1, source_target_pairs={{0,2},{1,3},{2,0},{3,1},{4,6},{5,7},{6,4},{7,5},{8,10},{9,11},{10,... | collective-permute-start | bytes 61448 | tf_op jit(solution)/shard_map/ppermute | solution.py:220
  8.7 1.8 %collective-permute-done.15 = bf16[2,80,64]{2,1,0:T(8,128)(2,1)S(1)} collective-permute-done((bf16[2,80,64]{2,1,0:T(8,128)(2,1)S(1)}, bf16[2,80,64]{2,1,0:T(8,128)(2,1)S(1)}, u32[]{:S(2)}, u32[]{:S(2)}) %collective-permute-start.15) | collective-permute-done | bytes 20512 | tf_op jit(solution)/shard_map/ppermute | solution.py:220
  10.7 2.5 %collective-permute-start.2 = (bf16[160,512]{1,0:T(8,128)(2,1)S(1)}, bf16[160,512]{1,0:T(8,128)(2,1)S(1)}, u32[]{:S(2)}, u32[]{:S(2)}) collective-permute-start(bf16[160,512]{1,0:T(8,128)(2,1)S(1)} %get-tuple-element.22), channel_id=1, source_target_pairs={{0,2},{1,3},{2,0},{3,1},{4,6},{5,7},{6,4},{7,5},{8,10},{9,11},{10,... | collective-permute-start | bytes 491528 | tf_op jit(solution)/shard_map/ppermute | solution.py:220
  13.2 2.6 %collective-permute-done.1 = bf16[160,512]{1,0:T(8,128)(2,1)S(1)} collective-permute-done((bf16[160,512]{1,0:T(8,128)(2,1)S(1)}, bf16[160,512]{1,0:T(8,128)(2,1)S(1)}, u32[]{:S(2)}, u32[]{:S(2)}) %collective-permute-start.1) | collective-permute-done | bytes 163872 | tf_op jit(solution)/shard_map/ppermute | solution.py:220
  15.8 1.6 %collective-permute-start.7 = (bf16[160,512]{1,0:T(8,128)(2,1)S(1)}, bf16[160,512]{1,0:T(8,128)(2,1)S(1)}, u32[]{:S(2)}, u32[]{:S(2)}) collective-permute-start(bf16[160,512]{1,0:T(8,128)(2,1)S(1)} %get-tuple-element.34), channel_id=1, source_target_pairs={{0,4},{4,0},{8,12},{12,8},{16,20},{20,16},{24,28},{28,24},{1,5},{5... | collective-permute-start | bytes 491528 | tf_op jit(solution)/shard_map/ppermute | solution.py:220
  17.4 1.6 %collective-permute-start.8 = (bf16[160,512]{1,0:T(8,128)(2,1)S(1)}, bf16[160,512]{1,0:T(8,128)(2,1)S(1)}, u32[]{:S(2)}, u32[]{:S(2)}) collective-permute-start(bf16[160,512]{1,0:T(8,128)(2,1)S(1)} %get-tuple-element.34), channel_id=1, source_target_pairs={{0,8},{4,12},{8,0},{12,4},{16,24},{20,28},{24,16},{28,20},{1,9},{5... | collective-permute-start | bytes 491528 | tf_op jit(solution)/shard_map/ppermute | solution.py:220
  19.0 2.6 %collective-permute-start.10 = (bf16[160,512]{1,0:T(8,128)(2,1)S(1)}, bf16[160,512]{1,0:T(8,128)(2,1)S(1)}, u32[]{:S(2)}, u32[]{:S(2)}) collective-permute-start(bf16[160,512]{1,0:T(8,128)(2,1)S(1)} %get-tuple-element.34), channel_id=1, source_target_pairs={{0,16},{4,20},{8,24},{12,28},{16,0},{20,4},{24,8},{28,12},{1,17},{... | collective-permute-start | bytes 491528 | tf_op jit(solution)/shard_map/ppermute | solution.py:220
  21.9 1.7 %collective-permute-done.8 = bf16[160,512]{1,0:T(8,128)(2,1)S(1)} collective-permute-done((bf16[160,512]{1,0:T(8,128)(2,1)S(1)}, bf16[160,512]{1,0:T(8,128)(2,1)S(1)}, u32[]{:S(2)}, u32[]{:S(2)}) %collective-permute-start.8) | collective-permute-done | bytes 163872 | tf_op jit(solution)/shard_map/ppermute | solution.py:220
  24.2 8.2 %collective-permute-done.10 = bf16[160,512]{1,0:T(8,128)(2,1)S(1)} collective-permute-done((bf16[160,512]{1,0:T(8,128)(2,1)S(1)}, bf16[160,512]{1,0:T(8,128)(2,1)S(1)}, u32[]{:S(2)}, u32[]{:S(2)}) %collective-permute-start.10) | collective-permute-done | bytes 163872 | tf_op jit(solution)/shard_map/ppermute | solution.py:220
  32.9 1.5 %collective-permute-start.13 = (bf16[160,512]{1,0:T(8,128)(2,1)S(1)}, bf16[160,512]{1,0:T(8,128)(2,1)S(1)}, u32[]{:S(2)}, u32[]{:S(2)}) collective-permute-start(bf16[160,512]{1,0:T(8,128)(2,1)S(1)} %collective-permute-done.12), channel_id=1, source_target_pairs={{0,4},{4,0},{8,12},{12,8},{16,20},{20,16},{24,28},{28,24},{1,5},{5... | collective-permute-start | bytes 491528 | tf_op jit(solution)/shard_map/ppermute | solution.py:220
  34.5 1.8 %shard_map.136 = (f32[1,32]{1,0:T(1,128)}, bf16[32,448]{1,0:T(8,128)(2,1)S(1)}) custom-call(s32[2]{0:T(128)S(1)} %pad_add_fusion.ids, bf16[32,64]{1,0:T(8,128)(2,1)S(1)} %copy-done.4, bf16[32,256]{1,0:T(8,128)(2,1)S(1)} %copy-done.3, bf16[2,160,512]{2,1,0:T(8,128)(2,1)S(1)} %pad_maximum_fusion.h_keep, ...), custom_call_target="tpu_custom_call" | custom-call | tf_op jit(solution)/shard_map/pallas_call | solution.py:209
  36.3 2.1 %shard_map.138 = bf16[80,512]{1,0:T(8,128)(2,1)S(1)} custom-call(s32[2]{0:T(128)S(1)} %pad_add_fusion.ids, bf16[32,64]{1,0:T(8,128)(2,1)S(1)} %copy-done.4, bf16[32,256]{1,0:T(8,128)(2,1)S(1)} %copy-done.3, bf16[32,448]{1,0:T(8,128)(2,1)S(1)} %get-tuple-element.25.info, bf16[2,160,512]{2,1,0:T(8,128)(2,1)S(1)} %pad_maximum_fusion.h_keep, ...), custom_call_target="tpu_custom_call" | custom-call | tf_op jit(solution)/shard_map/pallas_call | solution.py:209
  39.0 1.5 %collective-permute-start.4 = (bf16[1,32,448]{2,1,0:T(8,128)(2,1)S(1)}, bf16[1,32,448]{2,1,0:T(8,128)(2,1)S(1)}, u32[]{:S(2)}, u32[]{:S(2)}) collective-permute-start(bf16[1,32,448]{2,1,0:T(8,128)(2,1)S(1)} %bitcast.49), channel_id=1, source_target_pairs={{0,4},{4,0},{8,12},{12,8},{16,20},{20,16},{24,28},{28,24},{1,5},{5... | collective-permute-start | bytes 86024 | tf_op jit(solution)/shard_map/ppermute | solution.py:220
  40.6 2.6 %collective-permute-done.4 = bf16[1,32,448]{2,1,0:T(8,128)(2,1)S(1)} collective-permute-done((bf16[1,32,448]{2,1,0:T(8,128)(2,1)S(1)}, bf16[1,32,448]{2,1,0:T(8,128)(2,1)S(1)}, u32[]{:S(2)}, u32[]{:S(2)}) %collective-permute-start.4) | collective-permute-done | bytes 28704 | tf_op jit(solution)/shard_map/ppermute | solution.py:220
  43.3 1.5 %collective-permute-start.5 = (bf16[2,32,448]{2,1,0:T(8,128)(2,1)S(1)}, bf16[2,32,448]{2,1,0:T(8,128)(2,1)S(1)}, u32[]{:S(2)}, u32[]{:S(2)}) collective-permute-start(bf16[2,32,448]{2,1,0:T(8,128)(2,1)S(1)} %pad_maximum_fusion.3), channel_id=1, source_target_pairs={{0,8},{4,12},{8,0},{12,4},{16,24},{20,28},{24,16},{28,20},{1,9},{5... | collective-permute-start | bytes 172040 | tf_op jit(solution)/shard_map/ppermute | solution.py:220
  45.5 3.2 %collective-permute-done.5 = bf16[2,32,448]{2,1,0:T(8,128)(2,1)S(1)} collective-permute-done((bf16[2,32,448]{2,1,0:T(8,128)(2,1)S(1)}, bf16[2,32,448]{2,1,0:T(8,128)(2,1)S(1)}, u32[]{:S(2)}, u32[]{:S(2)}) %collective-permute-start.5) | collective-permute-done | bytes 57376 | tf_op jit(solution)/shard_map/ppermute | solution.py:220
  48.7 2.2 %collective-permute-start.6 = (bf16[4,32,448]{2,1,0:T(8,128)(2,1)S(1)}, bf16[4,32,448]{2,1,0:T(8,128)(2,1)S(1)}, u32[]{:S(2)}, u32[]{:S(2)}) collective-permute-start(bf16[4,32,448]{2,1,0:T(8,128)(2,1)S(1)} %pad_maximum_fusion.2), channel_id=1, source_target_pairs={{0,16},{4,20},{8,24},{12,28},{16,0},{20,4},{24,8},{28,12},{1,17},{... | collective-permute-start | bytes 344072 | tf_op jit(solution)/shard_map/ppermute | solution.py:220
  50.9 1.5 %collective-permute-start.21 = (bf16[80,512]{1,0:T(8,128)(2,1)S(1)}, bf16[80,512]{1,0:T(8,128)(2,1)S(1)}, u32[]{:S(2)}, u32[]{:S(2)}) collective-permute-start(bf16[80,512]{1,0:T(8,128)(2,1)S(1)} %add_convert_fusion.4.refs_4_), channel_id=1, source_target_pairs={{0,16},{4,20},{8,24},{12,28},{16,0},{20,4},{24,8},{28,12},{1,17},{... | collective-permute-start | bytes 245768 | tf_op jit(solution)/shard_map/ppermute | solution.py:220
  52.4 3.6 %collective-permute-done.6 = bf16[4,32,448]{2,1,0:T(8,128)(2,1)S(1)} collective-permute-done((bf16[4,32,448]{2,1,0:T(8,128)(2,1)S(1)}, bf16[4,32,448]{2,1,0:T(8,128)(2,1)S(1)}, u32[]{:S(2)}, u32[]{:S(2)}) %collective-permute-start.6) | collective-permute-done | bytes 114720 | tf_op jit(solution)/shard_map/ppermute | solution.py:220
  56.0 4.2 %shard_map.137 = (bf16[4,64,512]{2,1,0:T(8,128)(2,1)S(1)}, f32[64,512]{1,0:T(8,128)}, f32[1,512]{1,0:T(1,128)}, f32[1,64]{1,0:T(1,128)}) custom-call(s32[2]{0:T(128)S(1)} %pad_add_fusion.ids, bf16[8,32,448]{2,1,0:T(8,128)(2,1)S(1)} %pad_maximum_fusion.1.info, bf16[8,160,512]{2,1,0:T(8,128)(2,1)S(1)} %bitcast_dynamic-update-slice_fusion.hid, ...), custom_call_target="tpu_custom_call" | custom-call | tf_op jit(solution)/shard_map/pallas_call | solution.py:209
  60.4 1.3 %collective-permute-start.17 = (bf16[64,512]{1,0:T(8,128)(2,1)S(1)}, bf16[64,512]{1,0:T(8,128)(2,1)S(1)}, u32[]{:S(2)}, u32[]{:S(2)}) collective-permute-start(bf16[64,512]{1,0:T(8,128)(2,1)S(1)} %get-tuple-element.38), channel_id=1, source_target_pairs={{0,2},{1,3},{2,0},{3,1},{4,6},{5,7},{6,4},{7,5},{8,10},{9,11},{10,... | collective-permute-start | bytes 196616 | tf_op jit(solution)/shard_map/ppermute | solution.py:220
  62.2 2.8 %collective-permute-done.17.refs_2_ = bf16[64,512]{1,0:T(8,128)(2,1)S(1)} collective-permute-done((bf16[64,512]{1,0:T(8,128)(2,1)S(1)}, bf16[64,512]{1,0:T(8,128)(2,1)S(1)}, u32[]{:S(2)}, u32[]{:S(2)}) %collective-permute-start.17) | collective-permute-done | bytes 65568 | tf_op jit(solution)/shard_map/ppermute | solution.py:220
  66.1 1.4 %shard_map.139 = (f32[64,2048]{1,0:T(8,128)}, f32[64,512]{1,0:T(8,128)}, f32[1,512]{1,0:T(1,128)}) custom-call(s32[2]{0:T(128)S(1)} %pad_add_fusion.ids, bf16[64,512]{1,0:T(8,128)(2,1)S(1)} %get-tuple-element.40.refs_0_, bf16[64,512]{1,0:T(8,128)(2,1)S(1)} %collective-permute-done.16.refs_1_, bf16[64,512]{1,0:T(8,128)(2,1)S(1)} %collective-permute-done.17.refs_2_, ...), custom_call_target="tpu_custom_call" | custom-call | tf_op jit(solution)/shard_map/pallas_call | solution.py:209
  (67 shorter events, 7.0 us)
Async XLA Ops:
  3.7 4.8 %collective-permute-start = (bf16[2,160,512]{2,1,0:T(8,128)(2,1)S(1)}, bf16[2,160,512]{2,1,0:T(8,128)(2,1)S(1)}, u32[]{:S(2)}, u32[]{:S(2)}) collective-permute-start(bf16[2,160,512]{2,1,0:T(8,128)(2,1)S(1)} %get-tuple-element.21), channel_id=1, source_target_pairs={{0,1},{1,0},{2,3},{3,2},{4,5},{5,4},{6,7},{7,6},{8,9},{9,8},{10,11... | collective-permute-start | bytes 983048 | tf_op jit(solution)/shard_map/ppermute | solution.py:220
  4.5 1.3 %collective-permute-start.14 = (bf16[1,80,64]{2,1,0:T(8,128)(2,1)S(1)}, bf16[1,80,64]{2,1,0:T(8,128)(2,1)S(1)}, u32[]{:S(2)}, u32[]{:S(2)}) collective-permute-start(bf16[1,80,64]{2,1,0:T(8,128)(2,1)S(1)} %fusion.5), channel_id=1, source_target_pairs={{0,1},{1,0},{2,3},{3,2},{4,5},{5,4},{6,7},{7,6},{8,9},{9,8},{10,11... | collective-permute-start | bytes 30728 | tf_op jit(solution)/shard_map/ppermute | solution.py:220
  5.7 4.8 %collective-permute-start.15 = (bf16[2,80,64]{2,1,0:T(8,128)(2,1)S(1)}, bf16[2,80,64]{2,1,0:T(8,128)(2,1)S(1)}, u32[]{:S(2)}, u32[]{:S(2)}) collective-permute-start(bf16[2,80,64]{2,1,0:T(8,128)(2,1)S(1)} %pad_maximum_fusion.4), channel_id=1, source_target_pairs={{0,2},{1,3},{2,0},{3,1},{4,6},{5,7},{6,4},{7,5},{8,10},{9,11},{10,... | collective-permute-start | bytes 61448 | tf_op jit(solution)/shard_map/ppermute | solution.py:220
  8.6 7.1 %collective-permute-start.1 = (bf16[160,512]{1,0:T(8,128)(2,1)S(1)}, bf16[160,512]{1,0:T(8,128)(2,1)S(1)}, u32[]{:S(2)}, u32[]{:S(2)}) collective-permute-start(bf16[160,512]{1,0:T(8,128)(2,1)S(1)} %get-tuple-element.23), channel_id=1, source_target_pairs={{0,2},{1,3},{2,0},{3,1},{4,6},{5,7},{6,4},{7,5},{8,10},{9,11},{10,... | collective-permute-start | bytes 491528 | tf_op jit(solution)/shard_map/ppermute | solution.py:220
  10.6 23.9 %copy-start.4 = (bf16[32,64]{1,0:T(8,128)(2,1)S(1)}, bf16[32,64]{1,0:T(8,128)(2,1)}, u32[]{:S(2)}) copy-start(bf16[32,64]{1,0:T(8,128)(2,1)} %samples.5) | copy-start | bytes 12292
  10.6 23.9 %copy-start.5 = (bf16[2048]{0:T(1024)(128)(2,1)S(1)}, bf16[2048]{0:T(1024)(128)(2,1)}, u32[]{:S(2)}) copy-start(bf16[2048]{0:T(1024)(128)(2,1)} %b_mid.5) | copy-start | bytes 12292
  10.7 11.1 %collective-permute-start.2 = (bf16[160,512]{1,0:T(8,128)(2,1)S(1)}, bf16[160,512]{1,0:T(8,128)(2,1)S(1)}, u32[]{:S(2)}, u32[]{:S(2)}) collective-permute-start(bf16[160,512]{1,0:T(8,128)(2,1)S(1)} %get-tuple-element.22), channel_id=1, source_target_pairs={{0,2},{1,3},{2,0},{3,1},{4,6},{5,7},{6,4},{7,5},{8,10},{9,11},{10,... | collective-permute-start | bytes 491528 | tf_op jit(solution)/shard_map/ppermute | solution.py:220
  15.8 18.6 %collective-permute-start.7 = (bf16[160,512]{1,0:T(8,128)(2,1)S(1)}, bf16[160,512]{1,0:T(8,128)(2,1)S(1)}, u32[]{:S(2)}, u32[]{:S(2)}) collective-permute-start(bf16[160,512]{1,0:T(8,128)(2,1)S(1)} %get-tuple-element.34), channel_id=1, source_target_pairs={{0,4},{4,0},{8,12},{12,8},{16,20},{20,16},{24,28},{28,24},{1,5},{5... | collective-permute-start | bytes 491528 | tf_op jit(solution)/shard_map/ppermute | solution.py:220
  17.4 6.3 %collective-permute-start.8 = (bf16[160,512]{1,0:T(8,128)(2,1)S(1)}, bf16[160,512]{1,0:T(8,128)(2,1)S(1)}, u32[]{:S(2)}, u32[]{:S(2)}) collective-permute-start(bf16[160,512]{1,0:T(8,128)(2,1)S(1)} %get-tuple-element.34), channel_id=1, source_target_pairs={{0,8},{4,12},{8,0},{12,4},{16,24},{20,28},{24,16},{28,20},{1,9},{5... | collective-permute-start | bytes 491528 | tf_op jit(solution)/shard_map/ppermute | solution.py:220
  19.0 13.4 %collective-permute-start.10 = (bf16[160,512]{1,0:T(8,128)(2,1)S(1)}, bf16[160,512]{1,0:T(8,128)(2,1)S(1)}, u32[]{:S(2)}, u32[]{:S(2)}) collective-permute-start(bf16[160,512]{1,0:T(8,128)(2,1)S(1)} %get-tuple-element.34), channel_id=1, source_target_pairs={{0,16},{4,20},{8,24},{12,28},{16,0},{20,4},{24,8},{28,12},{1,17},{... | collective-permute-start | bytes 491528 | tf_op jit(solution)/shard_map/ppermute | solution.py:220
  21.5 11.4 %collective-permute-start.12 = (bf16[160,512]{1,0:T(8,128)(2,1)S(1)}, bf16[160,512]{1,0:T(8,128)(2,1)S(1)}, u32[]{:S(2)}, u32[]{:S(2)}) collective-permute-start(bf16[160,512]{1,0:T(8,128)(2,1)S(1)} %get-tuple-element.34), channel_id=1, source_target_pairs={{0,24},{4,28},{8,16},{12,20},{16,8},{20,12},{24,0},{28,4},{1,25},{... | collective-permute-start | bytes 491528 | tf_op jit(solution)/shard_map/ppermute | solution.py:220
  21.9 12.6 %collective-permute-start.3 = (bf16[2,160,512]{2,1,0:T(8,128)(2,1)S(1)}, bf16[2,160,512]{2,1,0:T(8,128)(2,1)S(1)}, u32[]{:S(2)}, u32[]{:S(2)}) collective-permute-start(bf16[2,160,512]{2,1,0:T(8,128)(2,1)S(1)} %pad_maximum_fusion.h_keep), channel_id=1, source_target_pairs={{0,1},{1,0},{2,3},{3,2},{4,5},{5,4},{6,7},{7,6},{8,9},{9,8},{10,11... | collective-permute-start | bytes 983048 | tf_op jit(solution)/shard_map/ppermute | solution.py:220
  23.6 16.9 %collective-permute-start.9 = (bf16[160,512]{1,0:T(8,128)(2,1)S(1)}, bf16[160,512]{1,0:T(8,128)(2,1)S(1)}, u32[]{:S(2)}, u32[]{:S(2)}) collective-permute-start(bf16[160,512]{1,0:T(8,128)(2,1)S(1)} %collective-permute-done.8), channel_id=1, source_target_pairs={{0,4},{4,0},{8,12},{12,8},{16,20},{20,16},{24,28},{28,24},{1,5},{5... | collective-permute-start | bytes 491528 | tf_op jit(solution)/shard_map/ppermute | solution.py:220
  32.4 8.2 %collective-permute-start.11 = (bf16[160,512]{1,0:T(8,128)(2,1)S(1)}, bf16[160,512]{1,0:T(8,128)(2,1)S(1)}, u32[]{:S(2)}, u32[]{:S(2)}) collective-permute-start(bf16[160,512]{1,0:T(8,128)(2,1)S(1)} %collective-permute-done.10), channel_id=1, source_target_pairs={{0,4},{4,0},{8,12},{12,8},{16,20},{20,16},{24,28},{28,24},{1,5},{5... | collective-permute-start | bytes 491528 | tf_op jit(solution)/shard_map/ppermute | solution.py:220
  32.9 7.7 %collective-permute-start.13 = (bf16[160,512]{1,0:T(8,128)(2,1)S(1)}, bf16[160,512]{1,0:T(8,128)(2,1)S(1)}, u32[]{:S(2)}, u32[]{:S(2)}) collective-permute-start(bf16[160,512]{1,0:T(8,128)(2,1)S(1)} %collective-permute-done.12), channel_id=1, source_target_pairs={{0,4},{4,0},{8,12},{12,8},{16,20},{20,16},{24,28},{28,24},{1,5},{5... | collective-permute-start | bytes 491528 | tf_op jit(solution)/shard_map/ppermute | solution.py:220
  38.4 6.4 %collective-permute-start.19 = (bf16[80,512]{1,0:T(8,128)(2,1)S(1)}, bf16[80,512]{1,0:T(8,128)(2,1)S(1)}, u32[]{:S(2)}, u32[]{:S(2)}) collective-permute-start(bf16[80,512]{1,0:T(8,128)(2,1)S(1)} %shard_map.138), channel_id=1, source_target_pairs={{0,4},{4,0},{8,12},{12,8},{16,20},{20,16},{24,28},{28,24},{1,5},{5... | collective-permute-start | bytes 245768 | tf_op jit(solution)/shard_map/ppermute | solution.py:220
  39.0 4.3 %collective-permute-start.4 = (bf16[1,32,448]{2,1,0:T(8,128)(2,1)S(1)}, bf16[1,32,448]{2,1,0:T(8,128)(2,1)S(1)}, u32[]{:S(2)}, u32[]{:S(2)}) collective-permute-start(bf16[1,32,448]{2,1,0:T(8,128)(2,1)S(1)} %bitcast.49), channel_id=1, source_target_pairs={{0,4},{4,0},{8,12},{12,8},{16,20},{20,16},{24,28},{28,24},{1,5},{5... | collective-permute-start | bytes 86024 | tf_op jit(solution)/shard_map/ppermute | solution.py:220
  43.3 5.4 %collective-permute-start.5 = (bf16[2,32,448]{2,1,0:T(8,128)(2,1)S(1)}, bf16[2,32,448]{2,1,0:T(8,128)(2,1)S(1)}, u32[]{:S(2)}, u32[]{:S(2)}) collective-permute-start(bf16[2,32,448]{2,1,0:T(8,128)(2,1)S(1)} %pad_maximum_fusion.3), channel_id=1, source_target_pairs={{0,8},{4,12},{8,0},{12,4},{16,24},{20,28},{24,16},{28,20},{1,9},{5... | collective-permute-start | bytes 172040 | tf_op jit(solution)/shard_map/ppermute | solution.py:220
  44.8 6.1 %collective-permute-start.20 = (bf16[80,512]{1,0:T(8,128)(2,1)S(1)}, bf16[80,512]{1,0:T(8,128)(2,1)S(1)}, u32[]{:S(2)}, u32[]{:S(2)}) collective-permute-start(bf16[80,512]{1,0:T(8,128)(2,1)S(1)} %add_convert_fusion.5), channel_id=1, source_target_pairs={{0,8},{4,12},{8,0},{12,4},{16,24},{20,28},{24,16},{28,20},{1,9},{5... | collective-permute-start | bytes 245768 | tf_op jit(solution)/shard_map/ppermute | solution.py:220
  48.7 7.3 %collective-permute-start.6 = (bf16[4,32,448]{2,1,0:T(8,128)(2,1)S(1)}, bf16[4,32,448]{2,1,0:T(8,128)(2,1)S(1)}, u32[]{:S(2)}, u32[]{:S(2)}) collective-permute-start(bf16[4,32,448]{2,1,0:T(8,128)(2,1)S(1)} %pad_maximum_fusion.2), channel_id=1, source_target_pairs={{0,16},{4,20},{8,24},{12,28},{16,0},{20,4},{24,8},{28,12},{1,17},{... | collective-permute-start | bytes 344072 | tf_op jit(solution)/shard_map/ppermute | solution.py:220
  50.9 11.3 %collective-permute-start.21 = (bf16[80,512]{1,0:T(8,128)(2,1)S(1)}, bf16[80,512]{1,0:T(8,128)(2,1)S(1)}, u32[]{:S(2)}, u32[]{:S(2)}) collective-permute-start(bf16[80,512]{1,0:T(8,128)(2,1)S(1)} %add_convert_fusion.4.refs_4_), channel_id=1, source_target_pairs={{0,16},{4,20},{8,24},{12,28},{16,0},{20,4},{24,8},{28,12},{1,17},{... | collective-permute-start | bytes 245768 | tf_op jit(solution)/shard_map/ppermute | solution.py:220
  60.3 1.9 %collective-permute-start.16 = (bf16[64,512]{1,0:T(8,128)(2,1)S(1)}, bf16[64,512]{1,0:T(8,128)(2,1)S(1)}, u32[]{:S(2)}, u32[]{:S(2)}) collective-permute-start(bf16[64,512]{1,0:T(8,128)(2,1)S(1)} %get-tuple-element.39), channel_id=1, source_target_pairs={{0,1},{1,0},{2,3},{3,2},{4,5},{5,4},{6,7},{7,6},{8,9},{9,8},{10,11... | collective-permute-start | bytes 196616 | tf_op jit(solution)/shard_map/ppermute | solution.py:220
  60.4 4.7 %collective-permute-start.17 = (bf16[64,512]{1,0:T(8,128)(2,1)S(1)}, bf16[64,512]{1,0:T(8,128)(2,1)S(1)}, u32[]{:S(2)}, u32[]{:S(2)}) collective-permute-start(bf16[64,512]{1,0:T(8,128)(2,1)S(1)} %get-tuple-element.38), channel_id=1, source_target_pairs={{0,2},{1,3},{2,0},{3,1},{4,6},{5,7},{6,4},{7,5},{8,10},{9,11},{10,... | collective-permute-start | bytes 196616 | tf_op jit(solution)/shard_map/ppermute | solution.py:220
  61.7 4.4 %collective-permute-start.18 = (bf16[64,512]{1,0:T(8,128)(2,1)S(1)}, bf16[64,512]{1,0:T(8,128)(2,1)S(1)}, u32[]{:S(2)}, u32[]{:S(2)}) collective-permute-start(bf16[64,512]{1,0:T(8,128)(2,1)S(1)} %get-tuple-element.37), channel_id=1, source_target_pairs={{0,3},{1,2},{2,1},{3,0},{4,7},{5,6},{6,5},{7,4},{8,11},{9,10},{10,... | collective-permute-start | bytes 196616 | tf_op jit(solution)/shard_map/ppermute | solution.py:220
  (6 other events, 99.6 us)
where the time goes:
time: 67.7 us; the launch traced here: 67.5 us
  waiting for transfers between devices  28.7 us (42%)
  starting transfers between devices  24.5 us (36%)
  Pallas kernels  12.5 us (18%)
  between operations  0.92 us (1%)
    ppermute x22, waiting for transfers between devices, xor_move(): lax.ppermute(x, axis, [(i, i ^ mask) for i in range(lax.axis_size(axis))])  28.7 us
    ppermute x22, starting transfers between devices, xor_move(): lax.ppermute(x, axis, [(i, i ^ mask) for i in range(lax.axis_size(axis))])  24.5 us
    pallas_call x5, Pallas kernels, call(): pl.pallas_call(body, in_specs=[pl.BlockSpec(memory_space=m) for m in spac...  12.5 us
  transfers between devices with their start and end apart: 22, of which 10 were waited for; matrix products, arithmetic and copies ran while one was open for 1% of the time, Pallas kernels for 12%

commit v1 on v0

--- a/solution.py
+++ b/solution.py
@@ -64,10 +64,49 @@
     return pre, signal
 
 
-def first_kernel(ids, samples, projections, w_in, b_in, w_mid, send, keep, w_buf, sems):
+def pack_weights(w_in, b_in, index, n_dp):
+    patch, width = w_in.shape
+    part, short = width // n_dp, patch // n_dp
+    row = lax.broadcasted_iota(jnp.int32, (width, part), 0)
+    col = lax.broadcasted_iota(jnp.int32, (width, part), 1)
+    pick = jnp.where(row == col + index * part, 1.0, 0.0).astype(BF16)
+    chosen = mm(w_in, pick, NN)
+    bias = mm(jnp.broadcast_to(b_in, (short, width)).astype(BF16), pick, NN)
+    wide = jnp.concatenate(rows_of(chosen, short), axis=1)
+    rest = jnp.concatenate([bias, jnp.zeros((short, width - part), F32)], axis=1)
+    return stack([wide, rest]).astype(BF16)
+
+
+def unpack_weights(packs, n_dp):
+    weights, biases = [], []
+    for pack in packs:
+        short = pack.shape[0] // 2
+        part = pack.shape[1] // n_dp
+        weights.append(stack(vectors_of(pack[:short], part)))
+        biases.append(pack[short : short + 1, :part])
+    return jnp.concatenate(weights, axis=1).astype(BF16), jnp.concatenate(biases, axis=1)
+
+
+def pack_inputs(inputs, out_rows, width):
+    short = 8
+    pieces = rows_of(inputs.astype(F32), short)
+    wide = width // inputs.shape[1]
+    pieces += [jnp.zeros_like(pieces[0])] * (out_rows // short * wide - len(pieces))
+    groups = [jnp.concatenate(pieces[i : i + wide], axis=1) for i in range(0, len(pieces), wide)]
+    return stack(groups).astype(BF16)
+
+
+def unpack_inputs(packed, full, patch):
+    short = 8
+    pieces = [v for group in rows_of(packed.astype(F32), short) for v in vectors_of(group, patch)]
+    return stack(pieces[: full // short]).astype(BF16)
+
+
+def first_kernel(n_dp, ids, samples, projections, w_in, b_in, w_mid, send, keep, known, w_buf, sems):
     me = ids[0]
     width = w_in.shape[1]
     n_blocks = w_buf.shape[0]
+    full = samples.shape[0] * (1 + projections.shape[1] // samples.shape[1])
     order = [*range(1, n_blocks, 2), *range(0, n_blocks, 2)]
     copies = []
     for r in order:
@@ -77,13 +116,19 @@
     inputs = input_rows(samples[...], projections[...])
     pieces = rows_of(mm(inputs, w_in[...], NN), samples.shape[0])
     layer = forward_layer(pieces, row_vector(b_in[...]))[0]
+    known[...] = pack_inputs(inputs, known.shape[0], width)
+    base = n_blocks // 2 * full
+    if send.shape[0] > base:
+        packed = pack_weights(w_in[...], row_vector(b_in[...]), ids[1], n_dp)
+        send[base:] = packed
+        keep[base:] = packed
     for r, copy in zip(order, copies):
         copy.wait()
         out = send if r % 2 else keep
-        out[r // 2] = mm(layer, w_buf[r], NN).astype(BF16)
-
-
-def score_kernel(ids, samples, projections, h_keep, h_recv, b_mid, w_out, b_out, loss, info, parts):
+        out[r // 2 * full : (r // 2 + 1) * full] = mm(layer, w_buf[r], NN).astype(BF16)
+
+
+def score_kernel(ids, projections, h_keep, h_recv, b_mid, w_out, b_out, loss, info, parts):
     me = ids[0]
     patch, width = w_out.shape[0], h_keep.shape[2]
     n_blocks = w_out.shape[1] // width
@@ -112,7 +157,7 @@
     loss[...] = jnp.sum(jnp.where(diagonal, losses, 0.0), axis=0, keepdims=True) / len(dirs)
     high = grad.astype(BF16)
     low = (grad - high.astype(F32)).astype(BF16)
-    info[...] = jnp.concatenate([high, low, samples[...], projections[...]], axis=1)
+    info[...] = jnp.concatenate([high, low], axis=1)
 
 
 def back_kernel(ids, samples, projections, info, h_keep, h_recv, b_mid, w_out, w_mid, w_in, b_in, out):
@@ -137,53 +182,82 @@
     pre, signal = backward_layer(rows_of(back_first, rows), pieces[1:], slopes, curv)
     out[:patch] = mm(inputs, signal, TN).astype(BF16)
     bias = jnp.sum(pre, axis=0, keepdims=True)
-    out[patch:] = jnp.broadcast_to(bias, (out.shape[0] - patch, width)).astype(BF16)
-
-
-def grads_kernel(ids, info, hid, b_mid, w_out, w_sel, block_out, g_out, g_mid, g_bias, acc, acc_mid, acc_bias):
-    n_dp, rows, span = info.shape
+    high = info[:, :patch].astype(F32)
+    score = jnp.sum(high + info[:, patch:].astype(F32), axis=0, keepdims=True)
+    score = jnp.concatenate([score, jnp.zeros((1, width - patch), F32)], axis=1)
+    short = (out.shape[0] - patch) // 2
+    wide = jnp.concatenate(rows_of(high, short), axis=1)
+    wide = jnp.concatenate([wide, jnp.zeros((short, width - wide.shape[1]), F32)], axis=1)
+    out[patch:] = stack([bias, score, jnp.zeros((short - 2, width), F32), wide]).astype(BF16)
+
+
+def grads_kernel(scale, n_dp, rows, full, n_before, final, ids, scores, hid, b_mid, w_out, w_near, w_far, *refs):
+    count = hid.shape[0]
+    before, refs = refs[: 2 * n_before + min(n_before, 1)], refs[2 * n_before + min(n_before, 1) :]
+    acc, acc_out, acc_mid = refs[-3:]
     patch, width = w_out.shape[0], hid.shape[2]
-    n_blocks, part = block_out.shape[0], block_out.shape[1]
-    scale = 1.0 / (rows * n_dp * (span // patch - 3))
     cols = pl.ds(pl.multiple_of(ids[0] * width, width), width)
-    mask = ids[1] if pairwise_size(n_dp) else 0
     w_own = w_out[:, cols]
     b_own = row_vector(b_mid[cols])
-    b_sel = w_sel[patch : patch + 1].astype(F32)
-    acc[...] = jnp.zeros_like(acc)
-    g_out[...] = jnp.zeros_like(g_out)
-    acc_mid[...] = jnp.zeros_like(acc_mid)
-    acc_bias[...] = jnp.zeros_like(acc_bias)
-
-    def body(step, carry):
-        slot = step ^ mask
-        known = info[slot]
-        hl = known[:, : 2 * patch]
-        inputs = stack(vectors_of(known, patch)[2:])
-        out_rows = stack([hl[:, :patch], inputs[rows:]])
-        pieces = rows_of(hid[slot].astype(F32), rows)
+    paired = w_near.shape[1] == width
+    if paired:
+        pairs = w_near[...].astype(F32), w_far[...].astype(F32)
+        w_sel, b_sel = unpack_weights([p for pair in pairs for p in rows_of(pair, pair.shape[0] // 2)], n_dp)
+    else:
+        w_sel, b_sel = w_near[:patch], w_near[patch : patch + 1].astype(F32)
+
+    def terms(slot):
+        inputs = unpack_inputs(hid[slot, full:], full, patch)
+        groups = rows // scores.shape[1]
+        score = stack(vectors_of(scores[slot].astype(F32), patch)[:groups]).astype(BF16)
+        out_rows = stack([score, inputs[rows:]])
+        pieces = rows_of(hid[slot, :full].astype(F32), rows)
         layer_two, slopes, curv = forward_layer(pieces, b_own)
         back = rows_of(mm(out_rows, w_own, NN), rows)
         pre, signal = backward_layer(back, pieces[1:], slopes, curv)
-        layer_one = forward_layer(rows_of(mm(inputs, w_sel[:patch], NN), rows), b_sel)[0]
-        acc[...] += mm(layer_one, signal, TN)
-        g_out[...] += mm(out_rows, layer_two, TN)
-        acc_mid[...] += pre
-        acc_bias[...] += hl.astype(F32)
-        return carry
-
-    lax.fori_loop(0, n_dp, body, 0, unroll=n_dp <= 8)
-    g_out[...] = g_out[...] * scale
-    g_mid[...] = jnp.sum(acc_mid[...], axis=0, keepdims=True) * scale
-    both = jnp.sum(acc_bias[...], axis=0, keepdims=True)
-    g_bias[...] = (both[:, :patch] + both[:, patch:]) * scale
+        layer_one = forward_layer(rows_of(mm(inputs, w_sel, NN), rows), b_sel)[0]
+        return mm(layer_one, signal, TN), mm(out_rows, layer_two, TN), pre
+
+    if paired:
+        mask = ids[1] & (count - 1)
+        total = before[0][...] if n_before else None
+        folded = None
+        for step in range(0, count, 2):
+            one, two = terms(step ^ mask), terms((step + 1) ^ mask)
+            total = one[0] + two[0] if total is None else total + one[0] + two[0]
+            pair = one[1] + two[1], one[2] + two[2]
+            folded = pair if folded is None else (folded[0] + pair[0], folded[1] + pair[1])
+        acc[...] = total
+        acc_out[...], acc_mid[...] = folded
+    else:
+        for ref in (acc, acc_out, acc_mid):
+            ref[...] = jnp.zeros_like(ref)
+
+        def body(step, carry):
+            for ref, term in zip((acc, acc_out, acc_mid), terms(step)):
+                ref[...] += term
+            return carry
+
+        lax.fori_loop(0, count, body, 0)
+        if n_before:
+            acc[...] += before[0][...]
+    if not final:
+        return
+    block_out, g_out, g_mid = refs[:3]
+    n_blocks, part = block_out.shape[0], block_out.shape[1]
+    out, mid = acc_out[...], acc_mid[...]
+    for i in reversed(range(n_before)):
+        out = out + before[1 + 2 * i][...]
+        mid = mid + before[2 + 2 * i][...]
+    g_out[...] = out * scale
+    g_mid[...] = jnp.sum(mid, axis=0, keepdims=True) * scale
     for r in range(n_blocks):
         block_out[r] = (acc[r * part : (r + 1) * part] * scale).astype(BF16)
 
 
 def merge_kernel(scale, ids, *refs):
     me = ids[0]
-    *chunks, mine, other, out, g_in, g_bias = refs
+    *chunks, mine, other, out, g_in, g_bias, g_last = refs
     width = mine.shape[1]
     patch = g_in.shape[0]
     for r, ref in enumerate(chunks):
@@ -192,6 +266,7 @@
     total = (mine[...].astype(F32) + other[...].astype(F32)) * scale
     g_in[...] = total[:patch]
     g_bias[...] = total[patch : patch + 1]
+    g_last[...] = total[patch + 1 : patch + 2, :patch]
 
 
 def shape(dims, dtype):
@@ -220,17 +295,7 @@
     return lax.ppermute(x, axis, [(i, i ^ mask) for i in range(lax.axis_size(axis))])
 
 
-def pairwise_size(size):
-    return size <= 8 and size & (size - 1) == 0
-
-
-def pairwise(axis):
-    return pairwise_size(lax.axis_size(axis))
-
-
 def doubling_gather(x, axis):
-    if not pairwise(axis):
-        return lax.all_gather(x, axis)
     out = x[None]
     mask = 1
     while mask < lax.axis_size(axis):
@@ -239,27 +304,13 @@
     return out
 
 
-def bulk_gather(x, axis):
-    if not pairwise(axis):
-        return lax.all_gather(x, axis)
-    size = lax.axis_size(axis)
-    slots = {0: x}
-    for mask in (2, 4, 6):
-        if mask < size:
-            slots[mask] = xor_move(x, axis, mask)
-    for mask in list(slots):
-        slots[mask ^ 1] = xor_move(slots[mask], axis, 1)
-    return jnp.stack([slots[i] for i in range(size)], axis=0)
-
-
-def pair_sum(x, axis):
-    if not pairwise(axis):
-        return lax.psum(x.astype(F32), axis), jnp.zeros_like(x)
-    mask = 1
-    while 2 * mask < lax.axis_size(axis):
-        x = (x.astype(F32) + xor_move(x, axis, mask).astype(F32)).astype(BF16)
-        mask *= 2
-    return x, xor_move(x, axis, mask)
+def halves(x):
+    half = x.shape[0] // 2
+    return x[:half], x[half:]
+
+
+def add_low(a, b):
+    return (a.astype(F32) + b.astype(F32)).astype(BF16)
 
 
 def shards(samples, projections, weight_in, bias_in, weight_mid, bias_mid, weight_out, bias_out):
@@ -272,12 +323,15 @@
     part = width // n_dp
     scale = 1.0 / (rows * n_dp * count)
     half = n_t // 2
+    paired = n_dp == 8 and n_t == 4
     ids = jnp.stack([t, d]).astype(jnp.int32)
     w_out = weight_out.T
-
-    send, keep = call(
-        first_kernel,
-        [near_shape((half, full, width), BF16)] * 2,
+    extra = 2 * patch // n_dp if paired else 0
+
+    packs = -(-full * patch // width // 8) * 8
+    send, keep, inputs = call(
+        functools.partial(first_kernel, n_dp),
+        [near_shape((half * full + extra, width), BF16)] * 2 + [near_shape((packs, width), BF16)],
         (ids, samples, projections, weight_in, bias_in, weight_mid),
         [pltpu.VMEM((n_t, width, width), BF16), pltpu.SemaphoreType.DMA((n_t,))],
         raw=(5,),
@@ -285,51 +339,85 @@
     )
 
     got = xor_move(send, "tensor", 1)
-    chip = [(keep[i].astype(F32) + got[i].astype(F32)).astype(BF16) for i in range(half)]
-    chip = lax.optimization_barrier(chip)
+    chip = [add_low(k, g) for k, g in zip(rows_of(keep, full)[:half], rows_of(got, full)[:half])]
+    chip = list(lax.optimization_barrier(chip))
     hidden = [c.astype(F32) for c in chip]
-    for q in range(1, half):
-        for i in range(half):
-            hidden[i] = hidden[i] + xor_move(chip[i ^ q], "tensor", 2 * q).astype(F32)
-    own = hidden[0].astype(BF16)
+    if paired:
+        w_near = jnp.concatenate([keep[half * full :], got[half * full :]], axis=0)
+        hidden[0] = hidden[0] + xor_move(chip[1], "tensor", 2).astype(F32)
+        second = xor_move(jnp.concatenate([chip[0], w_near], axis=0), "tensor", 2)
+        hidden[1] = hidden[1] + second[:full].astype(F32)
+        w_far = second[full:]
+    else:
+        for q in range(1, half):
+            for i in range(half):
+                hidden[i] = hidden[i] + xor_move(chip[i ^ q], "tensor", 2 * q).astype(F32)
+        sel = jnp.concatenate([weight_in, bias_in[None, :], jnp.zeros((15, width), BF16)], axis=0)
+        sel = doubling_gather(lax.dynamic_slice_in_dim(sel, d * part, part, 1), "tensor")
+        w_near = jnp.concatenate([sel[r] for r in range(n_t)], axis=1)
+        w_far = w_near
+    own = jnp.concatenate([hidden[0].astype(BF16), inputs], axis=0)
     h_keep = jnp.stack([h.astype(BF16) for h in hidden], axis=0)
     h_recv = xor_move(h_keep, "tensor", 1)
 
-    sel = jnp.concatenate([weight_in, bias_in[None, :], jnp.zeros((15, width), BF16)], axis=0)
-    sel = doubling_gather(lax.dynamic_slice_in_dim(sel, d * part, part, 1), "tensor")
-    w_sel = jnp.concatenate([sel[r] for r in range(n_t)], axis=1)
-
-    hid_all = bulk_gather(own, "dp")
-
     loss, info = call(
         score_kernel,
-        [shape((1, rows), F32), near_shape((rows, (3 + count) * patch), BF16)],
-        (ids, samples, projections, h_keep, h_recv, bias_mid, w_out, bias_out),
+        [shape((1, rows), F32), near_shape((rows, 2 * patch), BF16)],
+        (ids, projections, h_keep, h_recv, bias_mid, w_out, bias_out),
         [pltpu.VMEM((n_t, full, patch), F32)],
-        near=(3, 4, 6),
-    )
-    info_all = doubling_gather(info, "dp")
-
-    (summed,) = call(
+        near=(2, 3, 5),
+    )
+
+    (known,) = call(
         back_kernel,
         [near_shape((patch + 16, width), BF16)],
         (ids, samples, projections, info, h_keep, h_recv, bias_mid, w_out, weight_mid, weight_in, bias_in),
         near=(3, 4, 5, 7, 8),
     )
 
-    mid_block, g_out, g_mid, g_bias = call(
-        grads_kernel,
-        [near_shape((n_t, part, width), BF16), shape((patch, width), F32), shape((1, width), F32), shape((1, patch), F32)],
-        (ids, info_all, hid_all, bias_mid, w_out, w_sel),
-        [pltpu.VMEM((n_t * part, width), F32), pltpu.VMEM((rows, width), F32), pltpu.VMEM((rows, 2 * patch), F32)],
-        near=(1, 2, 4, 5) if pairwise("dp") else (),
-    )
+    if paired:
+        slots = {0: own}
+        slots[4] = xor_move(own, "dp", 4)
+        slots[2] = xor_move(own, "dp", 2)
+        slots[6] = xor_move(slots[2], "dp", 4)
+        for i in range(0, n_dp, 2):
+            slots[i + 1] = xor_move(slots[i], "dp", 1)
+        hid_parts = [jnp.stack([slots[i] for i in band]) for band in BANDS]
+        edge = patch + 8
+        summed, scores = known[:edge], [known[edge:]]
+        for mask in (1, 2, 4):
+            other = xor_move(jnp.concatenate([summed] + scores, axis=0), "dp", mask)
+            last = summed, other[:edge]
+            scores = scores + rows_of(other[edge:], 8)
+            summed = add_low(*last)
+        score_parts = [jnp.stack([scores[i] for i in band]) for band in BANDS]
+    else:
+        hid_parts = halves(lax.all_gather(own, "dp"))
+        score_parts = halves(lax.all_gather(known[patch + 8 :], "dp"))
+        summed = lax.psum(known.astype(F32), "dp")
+        last = summed, jnp.zeros_like(summed)
+
+    accs = [(n_t * part, width), (patch, width), (rows, width)]
+    blocks = [near_shape((n_t, part, width), BF16), shape((patch, width), F32), shape((1, width), F32)]
+    near = (1, 2, 4, 5, 6) if paired else ()
+    before = ()
+    for i, (hid, score) in enumerate(zip(hid_parts, score_parts)):
+        final = i + 1 == len(hid_parts)
+        results = call(
+            functools.partial(grads_kernel, scale, n_dp, rows, full, i, final),
+            blocks if final else [near_shape(dims, F32) for dims in accs],
+            (ids, score, hid, bias_mid, w_out, w_near, w_far, *before),
+            [pltpu.VMEM(dims, F32) for dims in accs] if final else [],
+            near=near + tuple(range(7, 7 + len(before))),
+        )
+        before = (results[0], *before[1:], *results[1:])
+    mid_block, g_out, g_mid = results
 
     chunks = [mid_block[0]] + [xor_move(mid_block[r], "tensor", r) for r in range(1, n_t)]
-    grad_mid, g_in, g_bias_in = call(
+    grad_mid, g_in, g_bias_in, g_bias_out = call(
         functools.partial(merge_kernel, scale),
-        [shape((part, n_t * width), F32), shape((patch, width), F32), shape((1, width), F32)],
-        (ids, *chunks, *pair_sum(summed, "dp")),
+        [shape((part, n_t * width), F32), shape((patch, width), F32), shape((1, width), F32), shape((1, patch), F32)],
+        (ids, *chunks, *last),
         near=tuple(range(1, n_t + 3)),
     )
     return (
@@ -339,8 +427,11 @@
         grad_mid,
         g_mid.reshape(width),
         g_out.T,
-        g_bias.reshape(patch),
-    )
+        g_bias_out.reshape(patch),
+    )
+
+
+BANDS = (range(4), range(4, 6), range(6, 8))
 
 
 def solution(mesh):

time: 67.7 us -> 64.5 us (0.953)
  starting transfers between devices: 24.5 us -> 17.5 us
  waiting for transfers between devices: 28.7 us -> 31.3 us
  Pallas kernels: 12.5 us -> 13.9 us
    ppermute x22 -> x17, starting transfers between devices: 24.5 us -> 17.5 us  [xor_move(): lax.ppermute(x, axis, [(i, i ^ mask) for i in range(lax.axis_size(axis))])]
    ppermute x22 -> x17, waiting for transfers between devices: 28.7 us -> 31.3 us  [xor_move(): lax.ppermute(x, axis, [(i, i ^ mask) for i in range(lax.axis_size(axis))])]
    pallas_call x5 -> x7, Pallas kernels: 12.5 us -> 13.9 us  [call(): pl.pallas_call(body, in_specs=[pl.BlockSpec(memory_space=m) for m in spac...]
  transfers between devices with their start and end apart: 22 -> 17, of which waited for: 10 -> 10; matrix products, arithmetic and copies ran while one was open for 1% -> 1% of each run, Pallas kernels for 12% -> 9%
where the time goes in v1:
time: 64.5 us; the launch traced here: 64.3 us
  waiting for transfers between devices  31.3 us (49%)
  starting transfers between devices  17.5 us (27%)
  Pallas kernels  13.9 us (22%)
  between operations  0.9 us (1%)
    ppermute x17, waiting for transfers between devices, xor_move(): lax.ppermute(x, axis, [(i, i ^ mask) for i in range(lax.axis_size(axis))])  31.3 us
    ppermute x17, starting transfers between devices, xor_move(): lax.ppermute(x, axis, [(i, i ^ mask) for i in range(lax.axis_size(axis))])  17.5 us
    pallas_call x7, Pallas kernels, call(): pl.pallas_call(body, in_specs=[pl.BlockSpec(memory_space=m) for m in spac...  13.9 us
  transfers between devices with their start and end apart: 17, of which 10 were waited for; matrix products, arithmetic and copies ran while one was open for 1% of the time, Pallas kernels for 9%

profile of v1, /device:TPU:0, one launch (start us, length us, event | category | flops | bytes accessed | tf_op | source)
XLA Modules:
  0.0 64.3 jit_solution(7338597040044794798)
XLA Ops:
  0.7 3.0 %shard_map.135 = (bf16[336,512]{1,0:T(8,128)(2,1)S(1)}, bf16[336,512]{1,0:T(8,128)(2,1)S(1)}, bf16[24,512]{1,0:T(8,128)(2,1)S(1)}) custom-call(s32[2]{0:T(128)S(1)} %pad_add_fusion.ids, bf16[32,64]{1,0:T(8,128)(2,1)} %samples.3, bf16[32,256]{1,0:T(8,128)(2,1)} %projections.5, bf16[64,512]{1,0:T(8,128)(2,1)} %w_in.3, bf16[512]{0:T(512)(128)(2,1)} %b_in.3, ...), custom_call_target="tpu_custom_call" | custom-call | tf_op jit(solution)/shard_map/pallas_call | solution.py:284
  4.3 1.3 %collective-permute-done = bf16[336,512]{1,0:T(8,128)(2,1)S(1)} collective-permute-done((bf16[336,512]{1,0:T(8,128)(2,1)S(1)}, bf16[336,512]{1,0:T(8,128)(2,1)S(1)}, u32[]{:S(2)}, u32[]{:S(2)}) %collective-permute-start) | collective-permute-done | bytes 344096 | tf_op jit(solution)/shard_map/ppermute | solution.py:295
  5.8 2.9 %collective-permute-start.1 = (bf16[160,512]{1,0:T(8,128)(2,1)S(1)}, bf16[160,512]{1,0:T(8,128)(2,1)S(1)}, u32[]{:S(2)}, u32[]{:S(2)}) collective-permute-start(bf16[160,512]{1,0:T(8,128)(2,1)S(1)} %get-tuple-element.30), channel_id=1, source_target_pairs={{0,2},{1,3},{2,0},{3,1},{4,6},{5,7},{6,4},{7,5},{8,10},{9,11},{10,... | collective-permute-start | bytes 491528 | tf_op jit(solution)/shard_map/ppermute | solution.py:295
  8.8 4.9 %collective-permute-done.1 = bf16[160,512]{1,0:T(8,128)(2,1)S(1)} collective-permute-done((bf16[160,512]{1,0:T(8,128)(2,1)S(1)}, bf16[160,512]{1,0:T(8,128)(2,1)S(1)}, u32[]{:S(2)}, u32[]{:S(2)}) %collective-permute-start.1) | collective-permute-done | bytes 163872 | tf_op jit(solution)/shard_map/ppermute | solution.py:295
  13.8 3.6 %collective-permute-done.2 = bf16[192,512]{1,0:T(8,128)(2,1)S(1)} collective-permute-done((bf16[192,512]{1,0:T(8,128)(2,1)S(1)}, bf16[192,512]{1,0:T(8,128)(2,1)S(1)}, u32[]{:S(2)}, u32[]{:S(2)}) %collective-permute-start.2) | collective-permute-done | bytes 196640 | tf_op jit(solution)/shard_map/ppermute | solution.py:295
  17.6 1.9 %collective-permute-start.7 = (bf16[184,512]{1,0:T(8,128)(2,1)S(1)}, bf16[184,512]{1,0:T(8,128)(2,1)S(1)}, u32[]{:S(2)}, u32[]{:S(2)}) collective-permute-start(bf16[184,512]{1,0:T(8,128)(2,1)S(1)} %get-tuple-element.54), channel_id=1, source_target_pairs={{0,8},{4,12},{8,0},{12,4},{16,24},{20,28},{24,16},{28,20},{1,9},{5... | collective-permute-start | bytes 565256 | tf_op jit(solution)/shard_map/ppermute | solution.py:295
  19.5 2.6 %collective-permute-start.10 = (bf16[184,512]{1,0:T(8,128)(2,1)S(1)}, bf16[184,512]{1,0:T(8,128)(2,1)S(1)}, u32[]{:S(2)}, u32[]{:S(2)}) collective-permute-start(bf16[184,512]{1,0:T(8,128)(2,1)S(1)} %get-tuple-element.54), channel_id=1, source_target_pairs={{0,16},{4,20},{8,24},{12,28},{16,0},{20,4},{24,8},{28,12},{1,17},{... | collective-permute-start | bytes 565256 | tf_op jit(solution)/shard_map/ppermute | solution.py:295
  22.1 1.5 %collective-permute-start.12 = (bf16[184,512]{1,0:T(8,128)(2,1)S(1)}, bf16[184,512]{1,0:T(8,128)(2,1)S(1)}, u32[]{:S(2)}, u32[]{:S(2)}) collective-permute-start(bf16[184,512]{1,0:T(8,128)(2,1)S(1)} %get-tuple-element.54), channel_id=1, source_target_pairs={{0,4},{4,0},{8,12},{12,8},{16,20},{20,16},{24,28},{28,24},{1,5},{5... | collective-permute-start | bytes 565256 | tf_op jit(solution)/shard_map/ppermute | solution.py:295
  23.6 5.2 %collective-permute-done.7 = bf16[184,512]{1,0:T(8,128)(2,1)S(1)} collective-permute-done((bf16[184,512]{1,0:T(8,128)(2,1)S(1)}, bf16[184,512]{1,0:T(8,128)(2,1)S(1)}, u32[]{:S(2)}, u32[]{:S(2)}) %collective-permute-start.7) | collective-permute-done | bytes 188448 | tf_op jit(solution)/shard_map/ppermute | solution.py:295
  28.8 1.7 %collective-permute-start.13 = (bf16[184,512]{1,0:T(8,128)(2,1)S(1)}, bf16[184,512]{1,0:T(8,128)(2,1)S(1)}, u32[]{:S(2)}, u32[]{:S(2)}) collective-permute-start(bf16[184,512]{1,0:T(8,128)(2,1)S(1)} %collective-permute-done.7), channel_id=1, source_target_pairs={{0,4},{4,0},{8,12},{12,8},{16,20},{20,16},{24,28},{28,24},{1,5},{5... | collective-permute-start | bytes 565256 | tf_op jit(solution)/shard_map/ppermute | solution.py:295
  31.3 1.5 %collective-permute-start.11 = (bf16[184,512]{1,0:T(8,128)(2,1)S(1)}, bf16[184,512]{1,0:T(8,128)(2,1)S(1)}, u32[]{:S(2)}, u32[]{:S(2)}) collective-permute-start(bf16[184,512]{1,0:T(8,128)(2,1)S(1)} %collective-permute-done.10), channel_id=1, source_target_pairs={{0,4},{4,0},{8,12},{12,8},{16,20},{20,16},{24,28},{28,24},{1,5},{5... | collective-permute-start | bytes 565256 | tf_op jit(solution)/shard_map/ppermute | solution.py:295
  32.8 1.7 %shard_map.136 = (f32[1,32]{1,0:T(1,128)}, bf16[32,128]{1,0:T(8,128)(2,1)S(1)}) custom-call(s32[2]{0:T(128)S(1)} %pad_add_fusion.ids, bf16[32,256]{1,0:T(8,128)(2,1)S(1)} %copy-done.3, bf16[2,160,512]{2,1,0:T(8,128)(2,1)S(1)} %pad_maximum_fusion.3.h_keep, bf16[2,160,512]{2,1,0:T(8,128)(2,1)S(1)} %collective-permute-done.3.h_recv, ...), custom_call_target="tpu_custom_call" | custom-call | tf_op jit(solution)/shard_map/pallas_call | solution.py:284
  34.6 2.1 %shard_map.137 = bf16[80,512]{1,0:T(8,128)(2,1)S(1)} custom-call(s32[2]{0:T(128)S(1)} %pad_add_fusion.ids, bf16[32,64]{1,0:T(8,128)(2,1)S(1)} %copy-done.5, bf16[32,256]{1,0:T(8,128)(2,1)S(1)} %copy-done.3, bf16[32,128]{1,0:T(8,128)(2,1)S(1)} %get-tuple-element.32.info, bf16[2,160,512]{2,1,0:T(8,128)(2,1)S(1)} %pad_maximum_fusion.3.h_keep, ...), custom_call_target="tpu_custom_call" | custom-call | tf_op jit(solution)/shard_map/pallas_call | solution.py:284
  37.3 3.9 %collective-permute-done.8 = bf16[184,512]{1,0:T(8,128)(2,1)S(1)} collective-permute-done((bf16[184,512]{1,0:T(8,128)(2,1)S(1)}, bf16[184,512]{1,0:T(8,128)(2,1)S(1)}, u32[]{:S(2)}, u32[]{:S(2)}) %collective-permute-start.8) | collective-permute-done | bytes 188448 | tf_op jit(solution)/shard_map/ppermute | solution.py:295
  41.9 0.7 %collective-permute-start.5 = (bf16[88,512]{1,0:T(8,128)(2,1)S(1)}, bf16[88,512]{1,0:T(8,128)(2,1)S(1)}, u32[]{:S(2)}, u32[]{:S(2)}) collective-permute-start(bf16[88,512]{1,0:T(8,128)(2,1)S(1)} %pad_maximum_fusion.7), channel_id=1, source_target_pairs={{0,8},{4,12},{8,0},{12,4},{16,24},{20,28},{24,16},{28,20},{1,9},{5... | collective-permute-start | bytes 270344 | tf_op jit(solution)/shard_map/ppermute | solution.py:295
  42.6 3.9 %collective-permute-done.5 = bf16[88,512]{1,0:T(8,128)(2,1)S(1)} collective-permute-done((bf16[88,512]{1,0:T(8,128)(2,1)S(1)}, bf16[88,512]{1,0:T(8,128)(2,1)S(1)}, u32[]{:S(2)}, u32[]{:S(2)}) %collective-permute-start.5) | collective-permute-done | bytes 90144 | tf_op jit(solution)/shard_map/ppermute | solution.py:295
  47.0 2.0 %shard_map.138 = (f32[256,512]{1,0:T(8,128)S(1)}, f32[64,512]{1,0:T(8,128)S(1)}, f32[32,512]{1,0:T(8,128)S(1)}) custom-call(s32[2]{0:T(128)S(1)} %pad_add_fusion.ids, bf16[4,8,512]{2,1,0:T(8,128)(2,1)S(1)} %pad_maximum_fusion.9.scores, bf16[4,184,512]{2,1,0:T(8,128)(2,1)S(1)} %pad_maximum_fusion.hid, bf16[2048]{0:T(1024)(128)(2,1)S(1)} %copy-done.4, ...), custom_call_target="tpu_custom_call" | custom-call | tf_op jit(solution)/shard_map/pallas_call | solution.py:284
  49.1 4.3 %collective-permute-done.6 = bf16[104,512]{1,0:T(8,128)(2,1)S(1)} collective-permute-done((bf16[104,512]{1,0:T(8,128)(2,1)S(1)}, bf16[104,512]{1,0:T(8,128)(2,1)S(1)}, u32[]{:S(2)}, u32[]{:S(2)}) %collective-permute-start.6) | collective-permute-done | bytes 106528 | tf_op jit(solution)/shard_map/ppermute | solution.py:295
  53.4 1.5 %shard_map.139 = (f32[256,512]{1,0:T(8,128)S(1)}, f32[64,512]{1,0:T(8,128)S(1)}, f32[32,512]{1,0:T(8,128)S(1)}) custom-call(s32[2]{0:T(128)S(1)} %pad_add_fusion.ids, bf16[2,8,512]{2,1,0:T(8,128)(2,1)S(1)} %pad_maximum_fusion.11.scores, bf16[2,184,512]{2,1,0:T(8,128)(2,1)S(1)} %pad_maximum_fusion.2.hid, bf16[2048]{0:T(1024)(128)(2,1)S(1)} %copy-done.4, ...), custom_call_target="tpu_custom_call" | custom-call | tf_op jit(solution)/shard_map/pallas_call | solution.py:284
  54.9 2.2 %shard_map.140 = (bf16[4,64,512]{2,1,0:T(8,128)(2,1)S(1)}, f32[64,512]{1,0:T(8,128)}, f32[1,512]{1,0:T(1,128)}) custom-call(s32[2]{0:T(128)S(1)} %pad_add_fusion.ids, bf16[2,8,512]{2,1,0:T(8,128)(2,1)S(1)} %pad_maximum_fusion.10.scores, bf16[2,184,512]{2,1,0:T(8,128)(2,1)S(1)} %pad_maximum_fusion.1.hid, bf16[2048]{0:T(1024)(128)(2,1)S(1)} %copy-done.4, ...), custom_call_target="tpu_custom_call" | custom-call | tf_op jit(solution)/shard_map/pallas_call | solution.py:284
  57.1 1.6 %collective-permute-start.15 = (bf16[64,512]{1,0:T(8,128)(2,1)S(1)}, bf16[64,512]{1,0:T(8,128)(2,1)S(1)}, u32[]{:S(2)}, u32[]{:S(2)}) collective-permute-start(bf16[64,512]{1,0:T(8,128)(2,1)S(1)} %get-tuple-element.50), channel_id=1, source_target_pairs={{0,2},{1,3},{2,0},{3,1},{4,6},{5,7},{6,4},{7,5},{8,10},{9,11},{10,... | collective-permute-start | bytes 196616 | tf_op jit(solution)/shard_map/ppermute | solution.py:295
  59.0 2.4 %collective-permute-done.16.refs_3_ = bf16[64,512]{1,0:T(8,128)(2,1)S(1)} collective-permute-done((bf16[64,512]{1,0:T(8,128)(2,1)S(1)}, bf16[64,512]{1,0:T(8,128)(2,1)S(1)}, u32[]{:S(2)}, u32[]{:S(2)}) %collective-permute-start.16) | collective-permute-done | bytes 65568 | tf_op jit(solution)/shard_map/ppermute | solution.py:295
  61.4 1.5 %collective-permute-done.15.refs_2_ = bf16[64,512]{1,0:T(8,128)(2,1)S(1)} collective-permute-done((bf16[64,512]{1,0:T(8,128)(2,1)S(1)}, bf16[64,512]{1,0:T(8,128)(2,1)S(1)}, u32[]{:S(2)}, u32[]{:S(2)}) %collective-permute-start.15) | collective-permute-done | bytes 65568 | tf_op jit(solution)/shard_map/ppermute | solution.py:295
  62.9 1.4 %shard_map.141 = (f32[64,2048]{1,0:T(8,128)}, f32[64,512]{1,0:T(8,128)}, f32[1,512]{1,0:T(1,128)}, f32[1,64]{1,0:T(1,128)}) custom-call(s32[2]{0:T(128)S(1)} %pad_add_fusion.ids, bf16[64,512]{1,0:T(8,128)(2,1)S(1)} %get-tuple-element.52.refs_0_, bf16[64,512]{1,0:T(8,128)(2,1)S(1)} %collective-permute-done.14.refs_1_, ...), custom_call_target="tpu_custom_call" | custom-call | tf_op jit(solution)/shard_map/pallas_call | solution.py:284
  (61 shorter events, 4.2 us)
Async XLA Ops:
  3.7 29.1 %copy-start.1 = (bf16[2048,64]{0,1:T(8,128)(2,1)S(1)}, bf16[2048,64]{0,1:T(8,128)(2,1)}, u32[]{:S(2)}) copy-start(bf16[2048,64]{0,1:T(8,128)(2,1)} %param.14) | copy-start | bytes 786436
  3.7 29.1 %copy-start.3 = (bf16[32,256]{1,0:T(8,128)(2,1)S(1)}, bf16[32,256]{1,0:T(8,128)(2,1)}, u32[]{:S(2)}) copy-start(bf16[32,256]{1,0:T(8,128)(2,1)} %projections.5) | copy-start | bytes 49156
  3.7 29.1 %copy-start.4 = (bf16[2048]{0:T(1024)(128)(2,1)S(1)}, bf16[2048]{0:T(1024)(128)(2,1)}, u32[]{:S(2)}) copy-start(bf16[2048]{0:T(1024)(128)(2,1)} %b_mid.9) | copy-start | bytes 12292
  3.8 29.0 %copy-start.7 = (f32[64]{0:T(128)S(1)}, f32[64]{0:T(128)}, u32[]{:S(2)}) copy-start(f32[64]{0:T(128)} %b_out.1) | copy-start | bytes 772
  3.8 1.8 %collective-permute-start = (bf16[336,512]{1,0:T(8,128)(2,1)S(1)}, bf16[336,512]{1,0:T(8,128)(2,1)S(1)}, u32[]{:S(2)}, u32[]{:S(2)}) collective-permute-start(bf16[336,512]{1,0:T(8,128)(2,1)S(1)} %get-tuple-element.28), channel_id=1, source_target_pairs={{0,1},{1,0},{2,3},{3,2},{4,5},{5,4},{6,7},{7,6},{8,9},{9,8},{10,11... | collective-permute-start | bytes 1032200 | tf_op jit(solution)/shard_map/ppermute | solution.py:295
  5.7 28.9 %copy-start = (bf16[512,2048]{1,0:T(8,128)(2,1)S(1)}, bf16[512,2048]{1,0:T(8,128)(2,1)}, u32[]{:S(2)}) copy-start(bf16[512,2048]{1,0:T(8,128)(2,1)} %w_mid.3) | copy-start | bytes 6291460
  5.7 28.9 %copy-start.2 = (bf16[64,512]{1,0:T(8,128)(2,1)S(1)}, bf16[64,512]{1,0:T(8,128)(2,1)}, u32[]{:S(2)}) copy-start(bf16[64,512]{1,0:T(8,128)(2,1)} %w_in.3) | copy-start | bytes 196612
  5.7 28.8 %copy-start.5 = (bf16[32,64]{1,0:T(8,128)(2,1)S(1)}, bf16[32,64]{1,0:T(8,128)(2,1)}, u32[]{:S(2)}) copy-start(bf16[32,64]{1,0:T(8,128)(2,1)} %samples.3) | copy-start | bytes 12292
  5.8 8.0 %collective-permute-start.1 = (bf16[160,512]{1,0:T(8,128)(2,1)S(1)}, bf16[160,512]{1,0:T(8,128)(2,1)S(1)}, u32[]{:S(2)}, u32[]{:S(2)}) collective-permute-start(bf16[160,512]{1,0:T(8,128)(2,1)S(1)} %get-tuple-element.30), channel_id=1, source_target_pairs={{0,2},{1,3},{2,0},{3,1},{4,6},{5,7},{6,4},{7,5},{8,10},{9,11},{10,... | collective-permute-start | bytes 491528 | tf_op jit(solution)/shard_map/ppermute | solution.py:295
  8.7 8.7 %collective-permute-start.2 = (bf16[192,512]{1,0:T(8,128)(2,1)S(1)}, bf16[192,512]{1,0:T(8,128)(2,1)S(1)}, u32[]{:S(2)}, u32[]{:S(2)}) collective-permute-start(bf16[192,512]{1,0:T(8,128)(2,1)S(1)} %pad_maximum_fusion.4), channel_id=1, source_target_pairs={{0,2},{1,3},{2,0},{3,1},{4,6},{5,7},{6,4},{7,5},{8,10},{9,11},{10,... | collective-permute-start | bytes 589832 | tf_op jit(solution)/shard_map/ppermute | solution.py:295
  17.5 15.3 %collective-permute-start.3 = (bf16[2,160,512]{2,1,0:T(8,128)(2,1)S(1)}, bf16[2,160,512]{2,1,0:T(8,128)(2,1)S(1)}, u32[]{:S(2)}, u32[]{:S(2)}) collective-permute-start(bf16[2,160,512]{2,1,0:T(8,128)(2,1)S(1)} %pad_maximum_fusion.3.h_keep), channel_id=1, source_target_pairs={{0,1},{1,0},{2,3},{3,2},{4,5},{5,4},{6,7},{7,6},{8,9},{9,8},{10,11... | collective-permute-start | bytes 983048 | tf_op jit(solution)/shard_map/ppermute | solution.py:295
  17.6 11.2 %collective-permute-start.7 = (bf16[184,512]{1,0:T(8,128)(2,1)S(1)}, bf16[184,512]{1,0:T(8,128)(2,1)S(1)}, u32[]{:S(2)}, u32[]{:S(2)}) collective-permute-start(bf16[184,512]{1,0:T(8,128)(2,1)S(1)} %get-tuple-element.54), channel_id=1, source_target_pairs={{0,8},{4,12},{8,0},{12,4},{16,24},{20,28},{24,16},{28,20},{1,9},{5... | collective-permute-start | bytes 565256 | tf_op jit(solution)/shard_map/ppermute | solution.py:295
  19.5 11.8 %collective-permute-start.10 = (bf16[184,512]{1,0:T(8,128)(2,1)S(1)}, bf16[184,512]{1,0:T(8,128)(2,1)S(1)}, u32[]{:S(2)}, u32[]{:S(2)}) collective-permute-start(bf16[184,512]{1,0:T(8,128)(2,1)S(1)} %get-tuple-element.54), channel_id=1, source_target_pairs={{0,16},{4,20},{8,24},{12,28},{16,0},{20,4},{24,8},{28,12},{1,17},{... | collective-permute-start | bytes 565256 | tf_op jit(solution)/shard_map/ppermute | solution.py:295
  22.1 19.7 %collective-permute-start.12 = (bf16[184,512]{1,0:T(8,128)(2,1)S(1)}, bf16[184,512]{1,0:T(8,128)(2,1)S(1)}, u32[]{:S(2)}, u32[]{:S(2)}) collective-permute-start(bf16[184,512]{1,0:T(8,128)(2,1)S(1)} %get-tuple-element.54), channel_id=1, source_target_pairs={{0,4},{4,0},{8,12},{12,8},{16,20},{20,16},{24,28},{28,24},{1,5},{5... | collective-permute-start | bytes 565256 | tf_op jit(solution)/shard_map/ppermute | solution.py:295
  28.8 13.0 %collective-permute-start.13 = (bf16[184,512]{1,0:T(8,128)(2,1)S(1)}, bf16[184,512]{1,0:T(8,128)(2,1)S(1)}, u32[]{:S(2)}, u32[]{:S(2)}) collective-permute-start(bf16[184,512]{1,0:T(8,128)(2,1)S(1)} %collective-permute-done.7), channel_id=1, source_target_pairs={{0,4},{4,0},{8,12},{12,8},{16,20},{20,16},{24,28},{28,24},{1,5},{5... | collective-permute-start | bytes 565256 | tf_op jit(solution)/shard_map/ppermute | solution.py:295
  30.4 10.8 %collective-permute-start.8 = (bf16[184,512]{1,0:T(8,128)(2,1)S(1)}, bf16[184,512]{1,0:T(8,128)(2,1)S(1)}, u32[]{:S(2)}, u32[]{:S(2)}) collective-permute-start(bf16[184,512]{1,0:T(8,128)(2,1)S(1)} %collective-permute-done.7), channel_id=1, source_target_pairs={{0,16},{4,20},{8,24},{12,28},{16,0},{20,4},{24,8},{28,12},{1,17},{... | collective-permute-start | bytes 565256 | tf_op jit(solution)/shard_map/ppermute | solution.py:295
  31.3 11.3 %collective-permute-start.11 = (bf16[184,512]{1,0:T(8,128)(2,1)S(1)}, bf16[184,512]{1,0:T(8,128)(2,1)S(1)}, u32[]{:S(2)}, u32[]{:S(2)}) collective-permute-start(bf16[184,512]{1,0:T(8,128)(2,1)S(1)} %collective-permute-done.10), channel_id=1, source_target_pairs={{0,4},{4,0},{8,12},{12,8},{16,20},{20,16},{24,28},{28,24},{1,5},{5... | collective-permute-start | bytes 565256 | tf_op jit(solution)/shard_map/ppermute | solution.py:295
  36.7 5.1 %collective-permute-start.4 = (bf16[80,512]{1,0:T(8,128)(2,1)S(1)}, bf16[80,512]{1,0:T(8,128)(2,1)S(1)}, u32[]{:S(2)}, u32[]{:S(2)}) collective-permute-start(bf16[80,512]{1,0:T(8,128)(2,1)S(1)} %shard_map.137), channel_id=1, source_target_pairs={{0,4},{4,0},{8,12},{12,8},{16,20},{20,16},{24,28},{28,24},{1,5},{5... | collective-permute-start | bytes 245768 | tf_op jit(solution)/shard_map/ppermute | solution.py:295
  41.2 7.8 %collective-permute-start.9 = (bf16[184,512]{1,0:T(8,128)(2,1)S(1)}, bf16[184,512]{1,0:T(8,128)(2,1)S(1)}, u32[]{:S(2)}, u32[]{:S(2)}) collective-permute-start(bf16[184,512]{1,0:T(8,128)(2,1)S(1)} %collective-permute-done.8), channel_id=1, source_target_pairs={{0,4},{4,0},{8,12},{12,8},{16,20},{20,16},{24,28},{28,24},{1,5},{5... | collective-permute-start | bytes 565256 | tf_op jit(solution)/shard_map/ppermute | solution.py:295
  41.9 4.6 %collective-permute-start.5 = (bf16[88,512]{1,0:T(8,128)(2,1)S(1)}, bf16[88,512]{1,0:T(8,128)(2,1)S(1)}, u32[]{:S(2)}, u32[]{:S(2)}) collective-permute-start(bf16[88,512]{1,0:T(8,128)(2,1)S(1)} %pad_maximum_fusion.7), channel_id=1, source_target_pairs={{0,8},{4,12},{8,0},{12,4},{16,24},{20,28},{24,16},{28,20},{1,9},{5... | collective-permute-start | bytes 270344 | tf_op jit(solution)/shard_map/ppermute | solution.py:295
  46.5 6.8 %collective-permute-start.6 = (bf16[104,512]{1,0:T(8,128)(2,1)S(1)}, bf16[104,512]{1,0:T(8,128)(2,1)S(1)}, u32[]{:S(2)}, u32[]{:S(2)}) collective-permute-start(bf16[104,512]{1,0:T(8,128)(2,1)S(1)} %pad_maximum_fusion.6), channel_id=1, source_target_pairs={{0,16},{4,20},{8,24},{12,28},{16,0},{20,4},{24,8},{28,12},{1,17},{... | collective-permute-start | bytes 319496 | tf_op jit(solution)/shard_map/ppermute | solution.py:295
  57.0 4.4 %collective-permute-start.16 = (bf16[64,512]{1,0:T(8,128)(2,1)S(1)}, bf16[64,512]{1,0:T(8,128)(2,1)S(1)}, u32[]{:S(2)}, u32[]{:S(2)}) collective-permute-start(bf16[64,512]{1,0:T(8,128)(2,1)S(1)} %get-tuple-element.49), channel_id=1, source_target_pairs={{0,3},{1,2},{2,1},{3,0},{4,7},{5,6},{6,5},{7,4},{8,11},{9,10},{10,... | collective-permute-start | bytes 196616 | tf_op jit(solution)/shard_map/ppermute | solution.py:295
  57.1 5.8 %collective-permute-start.15 = (bf16[64,512]{1,0:T(8,128)(2,1)S(1)}, bf16[64,512]{1,0:T(8,128)(2,1)S(1)}, u32[]{:S(2)}, u32[]{:S(2)}) collective-permute-start(bf16[64,512]{1,0:T(8,128)(2,1)S(1)} %get-tuple-element.50), channel_id=1, source_target_pairs={{0,2},{1,3},{2,0},{3,1},{4,6},{5,7},{6,4},{7,5},{8,10},{9,11},{10,... | collective-permute-start | bytes 196616 | tf_op jit(solution)/shard_map/ppermute | solution.py:295
  58.7 4.2 %collective-permute-start.14 = (bf16[64,512]{1,0:T(8,128)(2,1)S(1)}, bf16[64,512]{1,0:T(8,128)(2,1)S(1)}, u32[]{:S(2)}, u32[]{:S(2)}) collective-permute-start(bf16[64,512]{1,0:T(8,128)(2,1)S(1)} %get-tuple-element.51), channel_id=1, source_target_pairs={{0,1},{1,0},{2,3},{3,2},{4,5},{5,4},{6,7},{7,6},{8,9},{9,8},{10,11... | collective-permute-start | bytes 196616 | tf_op jit(solution)/shard_map/ppermute | solution.py:295
  (1 other events, 28.8 us)
